TPU v7x, 128 devices: a whole 4x4x4 slice. The times are simulated.
128 devices in a mesh: ctx: 16 (over y, x), tp: 8 (over z, core).
Axes of the slice: x: 4, y: 4, z: 4, core: 2. Of those that a mesh axis runs over, the one named last changes fastest.
Arguments:
- queries: bfloat16 [8192, 64, 128], P('ctx', 'tp'), may hold values from -5 to 5
- own_keys: bfloat16 [8192, 8, 128], P('ctx', 'tp'), may hold values from -5 to 5
- own_values: bfloat16 [8192, 8, 128], P('ctx', 'tp'), may hold values from -5 to 5
- cache_keys: bfloat16 [8, 65536, 128], P('tp', 'ctx'), may hold values from -5 to 5
- cache_values: bfloat16 [8, 65536, 128], P('tp', 'ctx'), may hold values from -5 to 5
- selected: int32 [16, 8, 8], P('ctx', 'tp'), may hold values from 0 to 127, as said below
- out_weight: bfloat16 [8192, 8192], P('tp'), may hold values from -0.0625 to 0.0625
Outputs:
- mixed: bfloat16 [8192, 8192], P('ctx', 'tp')
Inputs may be any that keep to these rules, and one draw needn't show every extreme that they name: `selected`: for each query block and key head, 8 different cache blocks, each lying in the cache of a different index of ctx (blocks k * 8 to (k + 1) * 8 - 1 for index k), so that at most 1 of them lie in one index.
All inputs are finite; a program needn't handle non-finite values.
Results may differ from a plain program's by a relative error of at most 0.017.
Values may be sent and summed in bfloat16 or wider, within the bound.
No kernel may reach another device: no remote copies, remote signals or barrier semaphores. Data moves between devices by JAX's collectives and lax.ppermute only.
A program may use at most 192 MiB of HBM per device.

v0:
```python
import jax
import jax.numpy as jnp
from jax import lax
from jax.sharding import PartitionSpec as P

CAPB = 1


def attend(query_block, key_set, value_set):
    rows_count, heads_count, head_width = query_block.shape
    total_keys = key_set.shape[0]
    remote_count = total_keys - rows_count
    column = lax.broadcasted_iota(jnp.int32, (rows_count, total_keys), 1)
    row_index = lax.broadcasted_iota(jnp.int32, (rows_count, total_keys), 0)
    allowed = (column < remote_count) | (column - remote_count <= row_index)
    paired_all = jnp.transpose(query_block, (1, 0, 2)).reshape(
        heads_count // 2, 2, rows_count, head_width
    )

    def one_pair(paired):
        scores = jnp.einsum("gtd,kd->gtk", paired, key_set, preferred_element_type=jnp.float32)
        scores = scores * head_width ** (-0.5)
        scores = jnp.where(allowed[None], scores, -jnp.inf)
        largest = jnp.max(scores, axis=2, keepdims=True)
        powers = jnp.exp(scores - largest)
        weights = (powers / jnp.sum(powers, axis=2, keepdims=True)).astype(jnp.bfloat16)
        return jnp.einsum(
            "gtk,kd->gtd", weights, value_set, preferred_element_type=jnp.float32
        ).astype(jnp.bfloat16)

    result = lax.map(one_pair, paired_all).reshape(heads_count, rows_count, head_width)
    return jnp.transpose(result, (1, 0, 2))


def shards(queries, own_keys, own_values, cache_keys, cache_values, selected, out_weight):
    block_rows = queries.shape[0]
    kv_local = cache_keys.shape[0]
    head_width = cache_keys.shape[2]
    blocks_dev = cache_keys.shape[1] // block_rows
    picked = selected[0]
    picked_count = picked.shape[1]
    owner_count = lax.axis_size("ctx")
    head_range = jnp.arange(kv_local, dtype=jnp.int32)[:, None]
    owner_of = picked // blocks_dev
    inside = picked % blocks_dev
    earlier = jnp.arange(picked_count)[None, :] < jnp.arange(picked_count)[:, None]
    same_owner = owner_of[:, :, None] == owner_of[:, None, :]
    ranking = jnp.sum(same_owner & earlier[None], axis=2)
    local_ids = head_range * blocks_dev + inside
    owner_match = (
        owner_of[:, :, None, None] == jnp.arange(owner_count, dtype=jnp.int32)[None, None, :, None]
    )
    slot_match = ranking[:, :, None, None] == jnp.arange(CAPB, dtype=jnp.int32)[None, None, None, :]
    request = jnp.sum(jnp.where(owner_match & slot_match, local_ids[:, :, None, None], 0), axis=1)
    request = jnp.transpose(request, (1, 0, 2))
    flat_keys = cache_keys.reshape(kv_local * blocks_dev, block_rows, head_width)
    flat_values = cache_values.reshape(kv_local * blocks_dev, block_rows, head_width)
    wanted = lax.all_to_all(request, "ctx", split_axis=0, concat_axis=0, tiled=True)
    got_keys = lax.all_to_all(flat_keys[wanted], "ctx", split_axis=0, concat_axis=0, tiled=True)
    got_values = lax.all_to_all(flat_values[wanted], "ctx", split_axis=0, concat_axis=0, tiled=True)
    position = owner_of * CAPB + ranking
    kv_head = 0
    key_blocks = [
        got_keys[:, kv_head].reshape(owner_count * CAPB, block_rows, head_width)[position[kv_head]]
    ]
    value_blocks = [
        got_values[:, kv_head].reshape(owner_count * CAPB, block_rows, head_width)[
            position[kv_head]
        ]
    ]
    kv_head = 0
    key_set = jnp.concatenate(
        [key_blocks[kv_head].reshape(picked_count * block_rows, head_width), own_keys[:, kv_head]],
        axis=0,
    )
    value_set = jnp.concatenate(
        [
            value_blocks[kv_head].reshape(picked_count * block_rows, head_width),
            own_values[:, kv_head],
        ],
        axis=0,
    )
    outputs = attend(queries, key_set, value_set)
    attended = outputs.reshape(block_rows, queries.shape[1] * head_width)
    partial_term = jnp.dot(attended, out_weight, preferred_element_type=jnp.float32).astype(
        jnp.bfloat16
    )
    return (
        lax.psum_scatter(partial_term, "tp", scatter_dimension=1, tiled=True)
        .astype(jnp.float32)
        .astype(jnp.bfloat16)
    )


def solution(mesh):
    in_specs = (
        P("ctx", "tp", None),
        P("ctx", "tp", None),
        P("ctx", "tp", None),
        P("tp", "ctx", None),
        P("tp", "ctx", None),
        P("ctx", "tp", None),
        P("tp", None),
    )
    out_specs = P("ctx", "tp")
    return jax.shard_map(shards, mesh=mesh, in_specs=in_specs, out_specs=out_specs, check_vma=False)
```

profile of v0, /device:TPU:1, one launch (start us, length us, event | category | flops | bytes accessed | tf_op | source)
XLA Modules:
  0.0 301.6 jit_solution(14684828833790092271)
XLA Ops:
  6.5 0.8 and_select_fusion.3
  7.3 0.7 fusion.25
  8.0 0.2 convert_reduce_fusion
  8.1 0.1 select_reduce_fusion
  8.2 0.1 copy.18
  8.3 13.8 %all_to_all.15 = s32[16,1,1]{2,1,0:T(1,128)S(1)} all-to-all(s32[16,1,1]{2,1,0:T(1,128)S(1)} %copy.18), channel_id=1, replica_groups=mesh['ctx'=16,'tp'=8] {'ctx'}, dimensions={0} | all-to-all | bytes 128 | tf_op jit(solution)/shard_map/all_to_all | solution.py:58
  22.1 0.4 fusion.21
  22.5 2.1 gather_fusion
  24.6 3.8 %all-to-all-start.1 = ((bf16[16,1,1,512,128]{4,3,2,1,0:T(8,128)(2,1)}), bf16[16,1,1,512,128]{4,3,2,1,0:T(8,128)(2,1)S(1)}, u32[]{:S(2)}, u32[]{:S(2)}) async-start(bf16[16,1,1,512,128]{4,3,2,1,0:T(8,128)(2,1)} %bitcast.6), calls=%async_computation.1 | async-start | bytes 4194304 | tf_op jit(solution)/shard_map/all_to_all | solution.py:59
  28.5 2.2 gather_fusion.2
  30.7 24.9 %all-to-all-done.1 = bf16[16,1,1,512,128]{4,3,2,1,0:T(8,128)(2,1)S(1)} async-done(((bf16[16,1,1,512,128]{4,3,2,1,0:T(8,128)(2,1)}), bf16[16,1,1,512,128]{4,3,2,1,0:T(8,128)(2,1)S(1)}, u32[]{:S(2)}, u32[]{:S(2)}) %all-to-all-start.1) | async-done | bytes 2097184 | tf_op jit(solution)/shard_map/all_to_all | solution.py:59
  55.6 6.7 %all-to-all-start.2 = ((bf16[16,1,1,512,128]{4,3,2,1,0:T(8,128)(2,1)}), bf16[16,1,1,512,128]{4,3,2,1,0:T(8,128)(2,1)}, u32[]{:S(2)}, u32[]{:S(2)}) async-start(bf16[16,1,1,512,128]{4,3,2,1,0:T(8,128)(2,1)} %bitcast.14), calls=%async_computation.2 | async-start | bytes 4194304 | tf_op jit(solution)/shard_map/all_to_all | solution.py:60
  62.3 0.0 reduce-scatter.2.cloned.1.call-start
  62.3 1.4 copy.17
  63.7 0.0 copy-start.4
  63.7 0.0 copy-start.5
  63.8 1.6 gather_fusion.1
  65.4 23.3 %all-to-all-done.2 = bf16[16,1,1,512,128]{4,3,2,1,0:T(8,128)(2,1)} async-done(((bf16[16,1,1,512,128]{4,3,2,1,0:T(8,128)(2,1)}), bf16[16,1,1,512,128]{4,3,2,1,0:T(8,128)(2,1)}, u32[]{:S(2)}, u32[]{:S(2)}) %all-to-all-start.2) | async-done | bytes 2097184 | tf_op jit(solution)/shard_map/all_to_all | solution.py:60
  88.7 2.3 gather_fusion.3
  91.1 1.6 pad_maximum_fusion
  92.7 132.3 %while.11 = (s32[]{:T(128)}, bf16[4,2,512,128]{2,3,1,0:T(8,128)(2,1)}, bf16[4,2,512,128]{3,2,1,0:T(8,128)(2,1)S(1)}, bf16[4608,128]{1,0:T(8,128)(2,1)}, bf16[460...) while((s32[]{:T(128)}, ...), condition=%wide.region_5.6_spmd.clone, body=%wide.region_2.5_spmd.clone.sunk | while | flops 2458522112 | bytes 84180056 | solution.py:31
  92.7 3.9 %fusion.39 = f32[2,512,4608]{2,1,0:T(8,128)S(1)} fusion(bf16[4608,128]{1,0:T(8,128)(2,1)} %get-tuple-element.142, bf16[4,2,512,128]{3,2,1,0:T(8,128)(2,1)S(1)} %get-tuple-element.141, s32[]{:T(128)} %get-tuple-element.131), kind=kOutput, calls=%fused_computation.18.clone.1 | convolution fusion | flops 1207959552 | bytes 20316164 | tf_op jit(solution)/shard_map/while/body/eval_jaxpr/gtd,kd->gtk/dot_general | solution.py:21
  96.6 3.1 %fusion.40 = pred[512,4608]{1,0:T(8,128)(4,1)} fusion(s32[4608]{0:T(1024)S(1)} %get-tuple-element.144, pred[4608]{0:T(1024)(128)(4,1)S(1)} %get-tuple-element.145), kind=kLoop, calls=%fused_computation.13.clone.1 | loop fusion | flops 4718592 | bytes 2382336 | tf_op jit(solution)/shard_map/or | solution.py:15
  99.6 16.0 %fusion.41 = (f32[2,512]{1,0:T(2,128)S(1)}, f32[2,512,4608]{2,1,0:T(8,128)}) fusion(f32[2,512,4608]{2,1,0:T(8,128)S(1)} %fusion.39, pred[512,4608]{1,0:T(8,128)(4,1)} %fusion.40), kind=kOutput, calls=%fused_computation.62.clone.1 | output fusion | flops 28316160 | bytes 40112128 | tf_op jit(solution)/shard_map/while/body/eval_jaxpr/sub | solution.py:25
  115.6 9.3 %fusion.42 = bf16[1,2,512,128]{3,2,1,0:T(8,128)(2,1)S(1)} fusion(bf16[4608,128]{1,0:T(8,128)(2,1)} %get-tuple-element.143, f32[2,512,4608]{2,1,0:T(8,128)} %get-tuple-element.121, f32[2,512]{1,0:T(2,128)S(1)} %get-tuple-element.122), kind=kOutput, calls=%fused_computation.20.clone.1 | convolution fusion | flops 1217527808 | bytes 20320256 | tf_op jit(solution)/shard_map/while/body/eval_jaxpr/gtk,kd->gtd/dot_general | solution.py:27
  124.9 0.1 copy.23
  125.0 0.7 constant_dynamic-update-slice_fusion.2
  125.8 3.9 %fusion.39 = f32[2,512,4608]{2,1,0:T(8,128)S(1)} fusion(bf16[4608,128]{1,0:T(8,128)(2,1)} %get-tuple-element.142, bf16[4,2,512,128]{3,2,1,0:T(8,128)(2,1)S(1)} %get-tuple-element.141, s32[]{:T(128)} %get-tuple-element.131), kind=kOutput, calls=%fused_computation.18.clone.1 | convolution fusion | flops 1207959552 | bytes 20316164 | tf_op jit(solution)/shard_map/while/body/eval_jaxpr/gtd,kd->gtk/dot_general | solution.py:21
  129.6 3.1 %fusion.40 = pred[512,4608]{1,0:T(8,128)(4,1)} fusion(s32[4608]{0:T(1024)S(1)} %get-tuple-element.144, pred[4608]{0:T(1024)(128)(4,1)S(1)} %get-tuple-element.145), kind=kLoop, calls=%fused_computation.13.clone.1 | loop fusion | flops 4718592 | bytes 2382336 | tf_op jit(solution)/shard_map/or | solution.py:15
  132.7 16.0 %fusion.41 = (f32[2,512]{1,0:T(2,128)S(1)}, f32[2,512,4608]{2,1,0:T(8,128)}) fusion(f32[2,512,4608]{2,1,0:T(8,128)S(1)} %fusion.39, pred[512,4608]{1,0:T(8,128)(4,1)} %fusion.40), kind=kOutput, calls=%fused_computation.62.clone.1 | output fusion | flops 28316160 | bytes 40112128 | tf_op jit(solution)/shard_map/while/body/eval_jaxpr/sub | solution.py:25
  148.7 9.3 %fusion.42 = bf16[1,2,512,128]{3,2,1,0:T(8,128)(2,1)S(1)} fusion(bf16[4608,128]{1,0:T(8,128)(2,1)} %get-tuple-element.143, f32[2,512,4608]{2,1,0:T(8,128)} %get-tuple-element.121, f32[2,512]{1,0:T(2,128)S(1)} %get-tuple-element.122), kind=kOutput, calls=%fused_computation.20.clone.1 | convolution fusion | flops 1217527808 | bytes 20320256 | tf_op jit(solution)/shard_map/while/body/eval_jaxpr/gtk,kd->gtd/dot_general | solution.py:27
  158.0 0.1 copy.23
  158.1 0.7 constant_dynamic-update-slice_fusion.2
  158.8 3.9 %fusion.39 = f32[2,512,4608]{2,1,0:T(8,128)S(1)} fusion(bf16[4608,128]{1,0:T(8,128)(2,1)} %get-tuple-element.142, bf16[4,2,512,128]{3,2,1,0:T(8,128)(2,1)S(1)} %get-tuple-element.141, s32[]{:T(128)} %get-tuple-element.131), kind=kOutput, calls=%fused_computation.18.clone.1 | convolution fusion | flops 1207959552 | bytes 20316164 | tf_op jit(solution)/shard_map/while/body/eval_jaxpr/gtd,kd->gtk/dot_general | solution.py:21
  162.7 3.1 %fusion.40 = pred[512,4608]{1,0:T(8,128)(4,1)} fusion(s32[4608]{0:T(1024)S(1)} %get-tuple-element.144, pred[4608]{0:T(1024)(128)(4,1)S(1)} %get-tuple-element.145), kind=kLoop, calls=%fused_computation.13.clone.1 | loop fusion | flops 4718592 | bytes 2382336 | tf_op jit(solution)/shard_map/or | solution.py:15
  165.8 16.0 %fusion.41 = (f32[2,512]{1,0:T(2,128)S(1)}, f32[2,512,4608]{2,1,0:T(8,128)}) fusion(f32[2,512,4608]{2,1,0:T(8,128)S(1)} %fusion.39, pred[512,4608]{1,0:T(8,128)(4,1)} %fusion.40), kind=kOutput, calls=%fused_computation.62.clone.1 | output fusion | flops 28316160 | bytes 40112128 | tf_op jit(solution)/shard_map/while/body/eval_jaxpr/sub | solution.py:25
  181.7 9.3 %fusion.42 = bf16[1,2,512,128]{3,2,1,0:T(8,128)(2,1)S(1)} fusion(bf16[4608,128]{1,0:T(8,128)(2,1)} %get-tuple-element.143, f32[2,512,4608]{2,1,0:T(8,128)} %get-tuple-element.121, f32[2,512]{1,0:T(2,128)S(1)} %get-tuple-element.122), kind=kOutput, calls=%fused_computation.20.clone.1 | convolution fusion | flops 1217527808 | bytes 20320256 | tf_op jit(solution)/shard_map/while/body/eval_jaxpr/gtk,kd->gtd/dot_general | solution.py:27
  191.0 0.1 copy.23
  191.2 0.7 constant_dynamic-update-slice_fusion.2
  191.9 3.9 %fusion.39 = f32[2,512,4608]{2,1,0:T(8,128)S(1)} fusion(bf16[4608,128]{1,0:T(8,128)(2,1)} %get-tuple-element.142, bf16[4,2,512,128]{3,2,1,0:T(8,128)(2,1)S(1)} %get-tuple-element.141, s32[]{:T(128)} %get-tuple-element.131), kind=kOutput, calls=%fused_computation.18.clone.1 | convolution fusion | flops 1207959552 | bytes 20316164 | tf_op jit(solution)/shard_map/while/body/eval_jaxpr/gtd,kd->gtk/dot_general | solution.py:21
  195.8 3.1 %fusion.40 = pred[512,4608]{1,0:T(8,128)(4,1)} fusion(s32[4608]{0:T(1024)S(1)} %get-tuple-element.144, pred[4608]{0:T(1024)(128)(4,1)S(1)} %get-tuple-element.145), kind=kLoop, calls=%fused_computation.13.clone.1 | loop fusion | flops 4718592 | bytes 2382336 | tf_op jit(solution)/shard_map/or | solution.py:15
  198.9 16.0 %fusion.41 = (f32[2,512]{1,0:T(2,128)S(1)}, f32[2,512,4608]{2,1,0:T(8,128)}) fusion(f32[2,512,4608]{2,1,0:T(8,128)S(1)} %fusion.39, pred[512,4608]{1,0:T(8,128)(4,1)} %fusion.40), kind=kOutput, calls=%fused_computation.62.clone.1 | output fusion | flops 28316160 | bytes 40112128 | tf_op jit(solution)/shard_map/while/body/eval_jaxpr/sub | solution.py:25
  214.8 9.3 %fusion.42 = bf16[1,2,512,128]{3,2,1,0:T(8,128)(2,1)S(1)} fusion(bf16[4608,128]{1,0:T(8,128)(2,1)} %get-tuple-element.143, f32[2,512,4608]{2,1,0:T(8,128)} %get-tuple-element.121, f32[2,512]{1,0:T(2,128)S(1)} %get-tuple-element.122), kind=kOutput, calls=%fused_computation.20.clone.1 | convolution fusion | flops 1217527808 | bytes 20320256 | tf_op jit(solution)/shard_map/while/body/eval_jaxpr/gtk,kd->gtd/dot_general | solution.py:27
  224.1 0.1 copy.23
  224.3 0.7 constant_dynamic-update-slice_fusion.2
  225.0 14.8 %convolution_convert_fusion = bf16[512,8192]{1,0:T(8,128)(2,1)} fusion(bf16[512,1024]{0,1:T(8,128)(2,1)} %bitcast.84, bf16[1024,8192]{1,0:T(8,128)(2,1)} %param.15), kind=kOutput, calls=%fused_computation.27 | convolution fusion | flops 8594128896 | bytes 26214400 | tf_op jit(solution)/shard_map/dot_general | solution.py:85
  239.8 0.0 reduce-scatter.2.cloned.1.call-update
  239.8 54.9 %reduce-scatter.2.cloned.1.call-done = bf16[512,1024]{1,0:T(8,128)(2,1)} async-done(((bf16[512,8192]{1,0:T(8,128)(2,1)}), bf16[512,1024]{1,0:T(8,128)(2,1)}) %reduce-scatter.2.cloned.1.call-update) | async-done | bytes 1048592 | tf_op jit(solution)/shard_map/reduce_scatter | solution.py:89
  (19 shorter events, 0.1 us)
Async XLA Ops:
  6.5 16.0 %copy-start = (bf16[1,4096,128]{2,1,0:T(8,128)(2,1)S(1)}, bf16[1,4096,128]{2,1,0:T(8,128)(2,1)}, u32[]{:S(2)}) copy-start(bf16[1,4096,128]{2,1,0:T(8,128)(2,1)} %param.12) | copy-start | bytes 3145732
  24.6 3.9 %copy-start.2 = (bf16[1,4096,128]{2,1,0:T(8,128)(2,1)S(1)}, bf16[1,4096,128]{2,1,0:T(8,128)(2,1)}, u32[]{:S(2)}) copy-start(bf16[1,4096,128]{2,1,0:T(8,128)(2,1)} %param.13) | copy-start | bytes 3145732
  24.6 30.9 %all-to-all-start.1 = ((bf16[16,1,1,512,128]{4,3,2,1,0:T(8,128)(2,1)}), bf16[16,1,1,512,128]{4,3,2,1,0:T(8,128)(2,1)S(1)}, u32[]{:S(2)}, u32[]{:S(2)}) async-start(bf16[16,1,1,512,128]{4,3,2,1,0:T(8,128)(2,1)} %bitcast.6), calls=%async_computation.1 | async-start | bytes 4194304 | tf_op jit(solution)/shard_map/all_to_all | solution.py:59
  55.6 8.1 %copy-start.6 = (s32[1,1,8]{2,1,0:T(1,128)S(1)}, s32[1,1,8]{2,1,0:T(1,128)}, u32[]{:S(2)}) copy-start(s32[1,1,8]{2,1,0:T(1,128)} %param.14) | copy-start | bytes 100
  55.6 33.1 %all-to-all-start.2 = ((bf16[16,1,1,512,128]{4,3,2,1,0:T(8,128)(2,1)}), bf16[16,1,1,512,128]{4,3,2,1,0:T(8,128)(2,1)}, u32[]{:S(2)}, u32[]{:S(2)}) async-start(bf16[16,1,1,512,128]{4,3,2,1,0:T(8,128)(2,1)} %bitcast.14), calls=%async_computation.2 | async-start | bytes 4194304 | tf_op jit(solution)/shard_map/all_to_all | solution.py:60
  62.3 232.4 %reduce-scatter.2.cloned.1.call-start = ((), (), s32[]{:S(2)}) async-start(), calls=%async_computation.4 | async-start | bytes 9437184 | tf_op jit(solution)/shard_map/reduce_scatter | solution.py:89
  63.7 27.4 %copy-start.4 = (bf16[512,1,128]{2,0,1:T(8,128)(2,1)S(1)}, bf16[512,1,128]{2,0,1:T(8,128)(2,1)}, u32[]{:S(2)}) copy-start(bf16[512,1,128]{2,0,1:T(8,128)(2,1)} %param.10) | copy-start | bytes 393220
  63.7 27.4 %copy-start.5 = (bf16[512,1,128]{2,0,1:T(8,128)(2,1)S(1)}, bf16[512,1,128]{2,0,1:T(8,128)(2,1)}, u32[]{:S(2)}) copy-start(bf16[512,1,128]{2,0,1:T(8,128)(2,1)} %param.11) | copy-start | bytes 393220
  65.4 25.6 %copy-start.3 = (bf16[8,512,128]{2,1,0:T(8,128)(2,1)S(1)}, bf16[8,512,128]{2,1,0:T(8,128)(2,1)}, u32[]{:S(2)}) copy-start(bf16[8,512,128]{2,1,0:T(8,128)(2,1)} %gather_fusion.1) | copy-start | bytes 3145732
  239.8 54.9 %copy-start.1 = (bf16[1,4096,128]{2,1,0:T(8,128)(2,1)S(1)}, bf16[1,4096,128]{2,1,0:T(8,128)(2,1)}, u32[]{:S(2)}) copy-start(bf16[1,4096,128]{2,1,0:T(8,128)(2,1)} %param.12) | copy-start | bytes 3145732
Sparse Core Ops, SparseCore 0:
  239.9 54.7 reduce-scatter.1
where the time goes:
time: 302 us
  waiting for transfers between devices  103 us (34%)
  other arithmetic  79.8 us (26%)
  matrix products  67.5 us (22%)
  blocking collectives  13.8 us (5%)
  between operations  13.5 us (4%)
  local copies, waits for them, and re-layouts  13.2 us (4%)
  starting transfers between devices  10.6 us (4%)
    sub x4, other arithmetic, one_pair(): powers = jnp.exp(scores - largest)  63.9 us
    reduce_scatter x1, waiting for transfers between devices, shards(): lax.psum_scatter(partial_term, 'tp', scatter_dimension=1, tiled=True)  54.9 us
    dot_general x4, matrix products, one_pair(): jnp.einsum('gtk,kd->gtd', weights, value_set, preferred_element_type=jnp....  37.1 us
    all_to_all x1, waiting for transfers between devices, shards(): lax.all_to_all(flat_keys[wanted], 'ctx', split_axis=0, concat_axis=0, til...  24.9 us
    all_to_all x1, waiting for transfers between devices, shards(): lax.all_to_all(flat_values[wanted], 'ctx', split_axis=0, concat_axis=0, t...  23.3 us
    dot_general x4, matrix products, one_pair(): jnp.einsum('gtd,kd->gtk', paired, key_set, preferred_element_type=jnp.flo...  15.5 us
    dot_general x1, matrix products, shards(): jnp.dot(attended, out_weight, preferred_element_type=jnp.float32)  14.8 us
    all_to_all x1, blocking collectives, shards(): lax.all_to_all(request, 'ctx', split_axis=0, concat_axis=0, tiled=True)  13.8 us
  transfers between devices with their start and end apart: 3, of which 3 were waited for; matrix products, arithmetic and copies ran while one was open for 2% of the time, Pallas kernels for 0%

commit v1 on v0

v1 whole, which is shorter than its diff:
```python
import functools, math
import jax, jax.numpy as jnp
from jax import lax
from jax.experimental import pallas as pl
from jax.experimental.pallas import tpu as pltpu
from jax.sharding import PartitionSpec as P

C = 128 ** -0.5 * math.log2(math.e)
R = 512
H = 8


def attn_body(pos_ref, q_ref, k_ref, v_ref, *rest, sub, per, items, unroll, first, last, causal):
    rest = list(rest)
    if not first:
        acc_in, m_in = rest.pop(0), rest.pop(0)
    if last:
        o_ref = rest.pop(0)
        acc_ref, m_ref, s_ref = rest
    else:
        acc_ref, m_ref, s_ref = rest
    total = H * items
    ones = jnp.ones((sub, 128), jnp.bfloat16)

    def slot(j, i):
        return pos_ref[j * per + i]

    def scores(t, buf):
        h, j = t // items, t % items
        q = q_ref[h]
        for i in range(per):
            s_ref[buf, :, i * sub:(i + 1) * sub] = lax.dot_general(
                q, k_ref[slot(j, i)], (((1,), (1,)), ((), ())), preferred_element_type=jnp.float32)

    def step(t, buf, j_static):
        h, j = t // items, t % items
        s = s_ref[buf]
        if causal:
            row = lax.broadcasted_iota(jnp.int32, s.shape, 0)
            col = lax.broadcasted_iota(jnp.int32, s.shape, 1)
            s = jnp.where(col <= row, s, -1e30)
        m_blk = jnp.max(s, axis=1, keepdims=True)
        fresh = first and j_static == 0
        if fresh:
            m_new = jnp.broadcast_to(m_blk, (R, 128))
        else:
            m_old = m_in[h] if j_static == 0 else m_ref[h]
            m_new = jnp.maximum(m_old, m_blk)
        mc = m_new[:, :1] * C
        p = jnp.exp2(s * C - mc).astype(jnp.bfloat16)
        pv = None
        for i in range(per):
            ve = jnp.concatenate([v_ref[slot(j, i)], ones], axis=1)
            d = jnp.dot(p[:, i * sub:(i + 1) * sub], ve, preferred_element_type=jnp.float32)
            pv = d if pv is None else pv + d
        if not fresh:
            alpha = jnp.exp2((m_old - m_new) * C)
            a_old = acc_in[h] if j_static == 0 else acc_ref[h]
            pv = jnp.concatenate([a_old[:, :128] * alpha, a_old[:, 128:] * alpha], axis=1) + pv
        if last and j_static == items - 1:
            o_ref[:, pl.ds(pl.multiple_of(h * 128, 128), 128)] = (pv[:, :128] / pv[:, 128:]).astype(jnp.bfloat16)
        else:
            acc_ref[h] = pv
            m_ref[h] = m_new

    scores(0, 0)

    def body(g, _):
        for u in range(unroll):
            t = g * unroll + u
            scores(jnp.minimum(t + 1, total - 1), (u + 1) % 2)
            step(t, u % 2, u % items)
        return 0

    lax.fori_loop(0, total // unroll, body, 0)


def attn_call(pos, q, k, v, state=None, *, sub, per, items, unroll, last, causal=False):
    first = state is None
    kern = functools.partial(attn_body, sub=sub, per=per, items=items, unroll=unroll, first=first, last=last, causal=causal)
    vm = pl.BlockSpec(memory_space=pltpu.VMEM)
    keys = sub * per * items
    acc_s = jax.ShapeDtypeStruct((H, R, 256), jnp.float32)
    m_s = jax.ShapeDtypeStruct((H, R, 128), jnp.float32)
    args = [q, k, v]
    if not first:
        args += list(state)
    scr = [pltpu.VMEM((2, R, sub * per), jnp.float32)]
    if last:
        out_shape = jax.ShapeDtypeStruct((R, H * 128), jnp.bfloat16)
        out_specs = vm
        scr = [pltpu.VMEM((H, R, 256), jnp.float32), pltpu.VMEM((H, R, 128), jnp.float32)] + scr
    else:
        out_shape = (acc_s, m_s)
        out_specs = (vm, vm)
    return pl.pallas_call(
        kern, out_shape=out_shape,
        in_specs=[pl.BlockSpec(memory_space=pltpu.SMEM)] + [vm] * len(args), out_specs=out_specs,
        scratch_shapes=scr,
        compiler_params=pltpu.CompilerParams(vmem_limit_bytes=56 * 2**20),
        cost_estimate=pl.CostEstimate(flops=4 * H * R * keys * 128 , bytes_accessed=2 * keys * 256, transcendentals=H * R * keys),
    )(pos, *args)


def shards(queries, own_keys, own_values, cache_keys, cache_values, selected, out_weight):
    blocks_dev = cache_keys.shape[1] // R
    picked = selected[0, 0]
    owners = lax.axis_size("ctx")
    owner_of = picked // blocks_dev
    inside = picked % blocks_dev
    match = owner_of[:, None] == jnp.arange(owners, dtype=jnp.int32)[None, :]
    request = jnp.sum(jnp.where(match, inside[:, None], 0), axis=0)
    wanted = lax.all_to_all(request, "ctx", split_axis=0, concat_axis=0, tiled=True)
    flat_keys = cache_keys.reshape(blocks_dev, R, 128)
    flat_values = cache_values.reshape(blocks_dev, R, 128)
    got_keys = lax.all_to_all(flat_keys[wanted], "ctx", split_axis=0, concat_axis=0, tiled=True)
    got_values = lax.all_to_all(flat_values[wanted], "ctx", split_axis=0, concat_axis=0, tiled=True)
    q = jnp.transpose(queries, (1, 0, 2))
    zero = jnp.zeros((1,), jnp.int32)
    state = attn_call(zero, q, own_keys.reshape(1, R, 128), own_values.reshape(1, R, 128),
                      sub=512, per=1, items=1, unroll=2, last=False, causal=True)
    attended = attn_call(owner_of, q, got_keys, got_values, state,
                         sub=512, per=2, items=4, unroll=4, last=True)
    partial_term = jnp.dot(attended, out_weight, preferred_element_type=jnp.float32).astype(jnp.bfloat16)
    return lax.psum_scatter(partial_term, "tp", scatter_dimension=1, tiled=True)


def solution(mesh):
    in_specs = (
        P("ctx", "tp", None),
        P("ctx", "tp", None),
        P("ctx", "tp", None),
        P("tp", "ctx", None),
        P("tp", "ctx", None),
        P("ctx", "tp", None),
        P("tp", None),
    )
    return jax.shard_map(shards, mesh=mesh, in_specs=in_specs, out_specs=P("ctx", "tp"), check_vma=False)
```

time: 302 us -> 195 us (0.65)
  other arithmetic: 79.8 us -> 1.23 us
  matrix products: 67.5 us -> 14.7 us
  Pallas kernels: 0 us -> 35.1 us
  waiting for transfers between devices: 103 us -> 97.3 us
  local copies, waits for them, and re-layouts: 13.2 us -> 8.1 us
    sub x5 -> x0, other arithmetic: 63.9 us -> none  [the longest x4 63.9 us: one_pair(): powers = jnp.exp(scores - largest)]
    dot_general x8 -> x0, matrix products: 52.7 us -> none  [the longest x4 37.1 us: one_pair(): jnp.einsum('gtk,kd->gtd', weights, value_set, preferred_element_type=jnp....]
    pallas_call x0 -> x2, Pallas kernels: none -> 35.1 us  [attn_call(): pl.pallas_call(kern, out_shape=out_shape, in_specs=[pl.BlockSpec(memory_s...]
    or x4 -> x0, other arithmetic: 12.2 us -> none  [attend(): allowed = (column < remote_count) | (column - remote_count <= row_index)]
    all_to_all x1, waiting for transfers between devices: 24.9 us -> 19.2 us  [shards(): lax.all_to_all(flat_keys[wanted], 'ctx', split_axis=0, concat_axis=0, til...]
    gather x2 -> x0, local copies, waits for them, and re-layouts: 3.99 us -> none  [the longest x1 2.34 us: shards(): got_values[:, kv_head].reshape(owner_count * CAPB, block_rows, head_width)]
    unnamed x14 -> x9, local copies, waits for them, and re-layouts: 0.03 us -> 3.69 us
    dynamic_update_slice x8 -> x0, local copies, waits for them, and re-layouts: 3.48 us -> none  [attend(): lax.map(one_pair, paired_all).reshape(heads_count, rows_count, head_width)]
  transfers between devices with their start and end apart: 3 -> 3, of which waited for: 3 -> 3; matrix products, arithmetic and copies ran while one was open for 2% -> 2% of each run, Pallas kernels for 0% -> 4%
where the time goes in v1:
time: 195 us
  waiting for transfers between devices  97.3 us (50%)
  Pallas kernels  35.1 us (18%)
  matrix products  14.7 us (8%)
  blocking collectives  13.8 us (7%)
  between operations  13.4 us (7%)
  starting transfers between devices  11.1 us (6%)
  local copies, waits for them, and re-layouts  8.1 us (4%)
    reduce_scatter x1, waiting for transfers between devices, shards(): return lax.psum_scatter(partial_term, 'tp', scatter_dimension=1, tiled=True)  53.1 us
    pallas_call x2, Pallas kernels, attn_call(): pl.pallas_call(kern, out_shape=out_shape, in_specs=[pl.BlockSpec(memory_s...  35.1 us
    all_to_all x1, waiting for transfers between devices, shards(): lax.all_to_all(flat_values[wanted], 'ctx', split_axis=0, concat_axis=0, t...  25 us
    all_to_all x1, waiting for transfers between devices, shards(): lax.all_to_all(flat_keys[wanted], 'ctx', split_axis=0, concat_axis=0, til...  19.2 us
    dot_general x1, matrix products, shards(): jnp.dot(attended, out_weight, preferred_element_type=jnp.float32)  14.7 us
    all_to_all x1, blocking collectives, shards(): lax.all_to_all(request, 'ctx', split_axis=0, concat_axis=0, tiled=True)  13.8 us
    all_to_all x1, starting transfers between devices, shards(): lax.all_to_all(flat_keys[wanted], 'ctx', split_axis=0, concat_axis=0, til...  6.48 us
    all_to_all x1, starting transfers between devices, shards(): lax.all_to_all(flat_values[wanted], 'ctx', split_axis=0, concat_axis=0, t...  4.57 us
  transfers between devices with their start and end apart: 3, of which 3 were waited for; matrix products, arithmetic and copies ran while one was open for 2% of the time, Pallas kernels for 4%

profile of v1, /device:TPU:1, one launch (start us, length us, event | category | flops | bytes accessed | tf_op | source)
XLA Modules:
  0.0 194.7 jit_solution(8394619212850571294)
XLA Ops:
  6.5 0.0 copy-start
  6.5 0.8 and_select_fusion
  7.3 0.0 copy-start.3
  7.3 0.1 select_reduce_fusion
  7.4 0.1 copy.14
  7.5 13.8 %all_to_all.22 = s32[16,1,1]{2,1,0:T(1,128)S(1)} all-to-all(s32[16,1,1]{2,1,0:T(1,128)S(1)} %copy.14), channel_id=1, replica_groups=mesh['ctx'=16,'tp'=8] {'ctx'}, dimensions={0} | all-to-all | bytes 128 | tf_op jit(solution)/shard_map/all_to_all | solution.py:113
  21.3 0.4 reduce
  21.7 0.0 copy-done
  21.7 2.2 %gather_fusion.1 = bf16[16,512,128]{2,1,0:T(8,128)(2,1)} fusion(bf16[8,512,128]{2,1,0:T(8,128)(2,1)S(1)} %bitcast.29, s32[1024]{0:T(1024)S(1)} %pad_clamp_fusion), kind=kCustom, calls=%fused_computation.1 | custom fusion | bytes 4194368 | tf_op jit(solution)/shard_map/gather | solution.py:117
  23.8 0.0 copy-done.3
  23.8 0.0 copy-start.1
  23.8 4.6 %all-to-all-start.2 = ((bf16[16,512,128]{2,1,0:T(8,128)(2,1)}), bf16[16,512,128]{2,1,0:T(8,128)(2,1)}, u32[]{:S(2)}, u32[]{:S(2)}) async-start(bf16[16,512,128]{2,1,0:T(8,128)(2,1)} %gather_fusion.1), calls=%async_computation.2 | async-start | bytes 4194304 | tf_op jit(solution)/shard_map/all_to_all | solution.py:117
  28.4 0.0 copy-done.1
  28.4 2.2 %gather_fusion = bf16[16,512,128]{2,1,0:T(8,128)(2,1)} fusion(bf16[8,512,128]{2,1,0:T(8,128)(2,1)S(1)} %bitcast.30, s32[1024]{0:T(1024)S(1)} %pad_clamp_fusion), kind=kCustom, calls=%fused_computation | custom fusion | bytes 4194368 | tf_op jit(solution)/shard_map/gather | solution.py:116
  30.6 25.0 %all-to-all-done.2.v_ref = bf16[16,512,128]{2,1,0:T(8,128)(2,1)} async-done(((bf16[16,512,128]{2,1,0:T(8,128)(2,1)}), bf16[16,512,128]{2,1,0:T(8,128)(2,1)}, u32[]{:S(2)}, u32[]{:S(2)}) %all-to-all-start.2) | async-done | bytes 2097184 | tf_op jit(solution)/shard_map/all_to_all | solution.py:117
  55.5 6.5 %all-to-all-start.1 = ((bf16[16,512,128]{2,1,0:T(8,128)(2,1)}), bf16[16,512,128]{2,1,0:T(8,128)(2,1)S(1)}, u32[]{:S(2)}, u32[]{:S(2)}) async-start(bf16[16,512,128]{2,1,0:T(8,128)(2,1)} %gather_fusion), calls=%async_computation.1 | async-start | bytes 4194304 | tf_op jit(solution)/shard_map/all_to_all | solution.py:116
  62.0 0.0 reduce-scatter.2.cloned.1.call-start
  62.1 2.3 %copy.16 = bf16[512,8,128]{2,0,1:T(8,128)(2,1)} copy(bf16[512,8,128]{2,1,0:T(8,128)(2,1)} %param.7) | data formatting | bytes 2097152 | tf_op args[0]
  64.4 7.0 %shard_map.73 = (f32[8,512,256]{2,1,0:T(8,128)}, f32[8,512,128]{2,1,0:T(8,128)}) custom-call(s32[1]{0:T(128)} %constant.32.clone.1.pos_ref, bf16[8,512,128]{2,1,0:T(8,128)(2,1)} %bitcast.31, bf16[1,512,128]{2,1,0:T(8,128)(2,1)} %bitcast.34, bf16[1,512,128]{2,1,0:T(8,128)(2,1)} %bitcast.35), custom_call_target="tpu_custom_call" | custom-call | flops 1073741824 | bytes 262144 | tf_op jit(solution)/shard_map/pallas_call | solution.py:96
  71.5 19.2 %all-to-all-done.1.k_ref = bf16[16,512,128]{2,1,0:T(8,128)(2,1)S(1)} async-done(((bf16[16,512,128]{2,1,0:T(8,128)(2,1)}), bf16[16,512,128]{2,1,0:T(8,128)(2,1)S(1)}, u32[]{:S(2)}, u32[]{:S(2)}) %all-to-all-start.1) | async-done | bytes 2097184 | tf_op jit(solution)/shard_map/all_to_all | solution.py:116
  90.6 0.0 copy-start.2
  90.6 1.3 copy-done.2
  92.0 28.0 %shard_map.74 = bf16[512,1024]{1,0:T(8,128)(2,1)} custom-call(s32[8]{0:T(128)} %copy-done.3, bf16[8,512,128]{2,1,0:T(8,128)(2,1)} %bitcast.32, bf16[16,512,128]{2,1,0:T(8,128)(2,1)} %copy-done.2, bf16[16,512,128]{2,1,0:T(8,128)(2,1)} %all-to-all-done.2.v_ref, f32[8,512,256]{2,1,0:T(8,128)} %get-tuple-element.7.rest_0_, f32[8,512,128]{2,1,0:T(8,128)} %get-tuple-element.8.rest_1_), custom_call_target="tpu_custom_call" | custom-call | flops 8589934592 | bytes 2097152 | tf_op jit(solution)/shard_map/pallas_call | solution.py:96
  120.0 14.7 %convolution_convert_fusion = bf16[512,8192]{1,0:T(8,128)(2,1)} fusion(bf16[512,1024]{1,0:T(8,128)(2,1)} %shard_map.74, bf16[1024,8192]{1,0:T(8,128)(2,1)} %param.13), kind=kOutput, calls=%fused_computation.2 | convolution fusion | flops 8594128896 | bytes 26214400 | tf_op jit(solution)/shard_map/dot_general | solution.py:124
  134.7 0.0 reduce-scatter.2.cloned.1.call-update
  134.7 53.1 %reduce-scatter.2.cloned.1.call-done = bf16[512,1024]{1,0:T(8,128)(2,1)} async-done(((bf16[512,8192]{1,0:T(8,128)(2,1)}), bf16[512,1024]{1,0:T(8,128)(2,1)}) %reduce-scatter.2.cloned.1.call-update) | async-done | bytes 1048592 | tf_op jit(solution)/shard_map/reduce_scatter | solution.py:125
  (2 shorter events, 0.0 us)
Async XLA Ops:
  6.5 15.1 %copy-start = (bf16[1,4096,128]{2,1,0:T(8,128)(2,1)S(1)}, bf16[1,4096,128]{2,1,0:T(8,128)(2,1)}, u32[]{:S(2)}) copy-start(bf16[1,4096,128]{2,1,0:T(8,128)(2,1)} %param.11) | copy-start | bytes 3145732
  7.3 16.5 %copy-start.3 = (s32[8]{0:T(128)}, s32[8]{0:T(128)S(1)}, u32[]{:S(2)}) copy-start(s32[8]{0:T(128)S(1)} %get-tuple-element.10.pos_ref) | copy-start | bytes 100
  23.8 4.6 %copy-start.1 = (bf16[1,4096,128]{2,1,0:T(8,128)(2,1)S(1)}, bf16[1,4096,128]{2,1,0:T(8,128)(2,1)}, u32[]{:S(2)}) copy-start(bf16[1,4096,128]{2,1,0:T(8,128)(2,1)} %param.10) | copy-start | bytes 3145732
  23.8 31.7 %all-to-all-start.2 = ((bf16[16,512,128]{2,1,0:T(8,128)(2,1)}), bf16[16,512,128]{2,1,0:T(8,128)(2,1)}, u32[]{:S(2)}, u32[]{:S(2)}) async-start(bf16[16,512,128]{2,1,0:T(8,128)(2,1)} %gather_fusion.1), calls=%async_computation.2 | async-start | bytes 4194304 | tf_op jit(solution)/shard_map/all_to_all | solution.py:117
  55.5 35.1 %all-to-all-start.1 = ((bf16[16,512,128]{2,1,0:T(8,128)(2,1)}), bf16[16,512,128]{2,1,0:T(8,128)(2,1)S(1)}, u32[]{:S(2)}, u32[]{:S(2)}) async-start(bf16[16,512,128]{2,1,0:T(8,128)(2,1)} %gather_fusion), calls=%async_computation.1 | async-start | bytes 4194304 | tf_op jit(solution)/shard_map/all_to_all | solution.py:116
  62.0 125.8 %reduce-scatter.2.cloned.1.call-start = ((), (), s32[]{:S(2)}) async-start(), calls=%async_computation.4 | async-start | bytes 9437184 | tf_op jit(solution)/shard_map/reduce_scatter | solution.py:125
  90.6 1.4 copy-start.2
Sparse Core Ops, SparseCore 0:
  134.8 52.9 reduce-scatter.1

commit v2 on v1

v2 whole, which is shorter than its diff:
```python
import functools
import math

import jax
import jax.numpy as jnp
from jax import lax
from jax.experimental import pallas as pl
from jax.experimental.pallas import tpu as pltpu
from jax.sharding import PartitionSpec as P


C = 128 ** -0.5 * math.log2(math.e)
R = 512
H = 8
W = 128
CUT = 320
ATT = 58
MIB = 2**20
VM = pl.BlockSpec(memory_space=pltpu.VMEM)
SM = pl.BlockSpec(memory_space=pltpu.SMEM)


def cat(parts, axis):
    return parts[0] if len(parts) == 1 else jnp.concatenate(parts, axis=axis)


def attend_body(pos_ref, q_ref, *rest, per, items, group, own, last):
    rest = list(rest)
    if own:
        k_ref, v_ref = rest.pop(0), rest.pop(0)
    else:
        kv_ref, acc_in, m_in = rest.pop(0), rest.pop(0), rest.pop(0)
    if last:
        o_ref = rest.pop(0)
    acc_ref, m_ref, s_ref = rest
    g = pl.program_id(0)
    keys = s_ref.shape[2]
    steps = group * items

    def chunk(j, which):
        if own:
            return (v_ref if which else k_ref)[...]
        return cat([kv_ref[pos_ref[j * per + i], which] for i in range(per)], 0)

    def scores(head, j, buf):
        s_ref[buf] = lax.dot_general(
            q_ref[head], chunk(j, 0), (((1,), (1,)), ((), ())), preferred_element_type=jnp.float32
        )

    def step(r, j, buf):
        s = s_ref[buf]
        if own:
            row = lax.broadcasted_iota(jnp.int32, s.shape, 0)
            col = lax.broadcasted_iota(jnp.int32, s.shape, 1)
            s = jnp.where(col <= row, s, -1e30)
        m_blk = jnp.max(s, axis=1, keepdims=True)
        if own:
            m_new = jnp.broadcast_to(m_blk, (R, W))
        else:
            m_old = m_in[r] if j == 0 else m_ref[r]
            m_new = jnp.maximum(m_old, m_blk)
        p = jnp.exp2(s * C - m_new[:, :1] * C).astype(jnp.bfloat16)
        ve = jnp.concatenate([chunk(j, 1), jnp.ones((keys, W), jnp.bfloat16)], axis=1)
        pv = jnp.dot(p, ve, preferred_element_type=jnp.float32)
        if not own:
            alpha = jnp.exp2((m_old - m_new) * C)
            a_old = acc_in[r] if j == 0 else acc_ref[r]
            pv = jnp.concatenate([a_old[:, :W] * alpha, a_old[:, W:] * alpha], axis=1) + pv
        if last and j == items - 1:
            o_ref[:, r * W : (r + 1) * W] = (pv[:, :W] / pv[:, W:]).astype(jnp.bfloat16)
        else:
            acc_ref[r] = pv
            m_ref[r] = m_new

    @pl.when(g == 0)
    def _():
        scores(0, 0, 0)

    for u in range(steps):
        if u + 1 < steps:
            scores(g * group + (u + 1) // items, (u + 1) % items, (u + 1) % 2)
        else:
            scores(jnp.minimum((g + 1) * group, H - 1), 0, (u + 1) % 2)
        step(u // items, u % items, u % 2)


def attend(pos, q, arrays, *, per, items, width, group=2, own=False, last=False):
    keys = per * width
    acc = pl.BlockSpec((group, R, 2 * W), lambda g: (g, 0, 0))
    top = pl.BlockSpec((group, R, W), lambda g: (g, 0, 0))
    scratch = [pltpu.VMEM((2, R, keys), jnp.float32)]
    if last:
        out_shape = jax.ShapeDtypeStruct((R, H * W), jnp.bfloat16)
        out_specs = pl.BlockSpec((R, group * W), lambda g: (0, g))
        scratch = [pltpu.VMEM((group, R, 2 * W), jnp.float32), pltpu.VMEM((group, R, W), jnp.float32)] + scratch
    else:
        out_shape = (jax.ShapeDtypeStruct((H, R, 2 * W), jnp.float32), jax.ShapeDtypeStruct((H, R, W), jnp.float32))
        out_specs = (acc, top)
    return pl.pallas_call(
        functools.partial(attend_body, per=per, items=items, group=group, own=own, last=last),
        grid=(H // group,),
        out_shape=out_shape,
        in_specs=[SM, VM] + ([VM, VM] if own else [VM, acc, top]),
        out_specs=out_specs,
        scratch_shapes=scratch,
        compiler_params=pltpu.CompilerParams(vmem_limit_bytes=ATT * MIB),
        cost_estimate=pl.CostEstimate(
            flops=16 * H * R * keys * items * W, bytes_accessed=16 * MIB, transcendentals=H * R * keys * items
        ),
    )(pos, q, *arrays)


def gather_body(want_ref, k_ref, v_ref, a_ref, b_ref, sems):
    copies = []
    for i in range(a_ref.shape[0]):
        for which, ref in enumerate((k_ref, v_ref)):
            block = ref.at[want_ref[i]]
            copies.append(pltpu.make_async_copy(block.at[pl.ds(0, CUT)], a_ref.at[i, which], sems.at[i, which, 0]))
            copies.append(pltpu.make_async_copy(block.at[pl.ds(CUT, R - CUT)], b_ref.at[i, which], sems.at[i, which, 1]))
    for copy in copies:
        copy.start()
    for copy in copies:
        copy.wait()


def gather(want, keys, values):
    n = want.shape[0]
    hbm = pl.BlockSpec(memory_space=pltpu.HBM)
    return pl.pallas_call(
        gather_body,
        out_shape=(
            jax.ShapeDtypeStruct((n, 2, CUT, W), jnp.bfloat16),
            jax.ShapeDtypeStruct((n, 2, R - CUT, W), jnp.bfloat16),
        ),
        in_specs=[SM, VM, VM],
        out_specs=(hbm, hbm),
        scratch_shapes=[pltpu.SemaphoreType.DMA((n, 2, 2))],
        compiler_params=pltpu.CompilerParams(vmem_limit_bytes=16 * MIB),
        cost_estimate=pl.CostEstimate(flops=0, bytes_accessed=8 * MIB, transcendentals=0),
    )(want, keys, values)


def copy_body(ix_ref, i_ref, o_ref):
    o_ref[...] = i_ref[...]


def sibling_columns(weight, side):
    rows = weight.shape[0]
    return pl.pallas_call(
        copy_body,
        grid_spec=pltpu.PrefetchScalarGridSpec(
            num_scalar_prefetch=1,
            grid=(4,),
            in_specs=[pl.BlockSpec((rows, 1024), lambda n, ix: (0, 2 * n + ix[0]))],
            out_specs=pl.BlockSpec((rows, 1024), lambda n, ix: (0, n)),
        ),
        out_shape=jax.ShapeDtypeStruct((rows, 4096), jnp.bfloat16),
        compiler_params=pltpu.CompilerParams(vmem_limit_bytes=60 * MIB),
        cost_estimate=pl.CostEstimate(flops=0, bytes_accessed=16 * MIB, transcendentals=0),
    )(side, weight)


def project_body(j_ref, a_ref, b_ref, w_ref, ws_ref, *rest, pieces, received):
    outs = rest[received : received + 2]
    buf, sems = rest[received + 2 :]
    z, c = j_ref[0] // 2, j_ref[0] % 2

    def fetch(n, part):
        d, half = pieces[n // 2]
        zz = (z + d) % 4
        ref = ws_ref if part else w_ref
        first = zz * 4 + 2 * half if part else (2 * zz + c) * 4 + 2 * half
        start = pl.multiple_of((first + n % 2) * 256, 256)
        return pltpu.make_async_copy(ref.at[:, pl.ds(start, 256)], buf.at[n, part], sems.at[n, part])

    for n in range(4):
        for part in range(2):
            fetch(n, part).start()
    for half in range(2):

        def one(m, carry):
            n = half * 2 + m
            for part in range(2):
                pltpu.make_async_copy(w_ref.at[:, pl.ds(0, 256)], buf.at[n, part], sems.at[n, part]).wait()
            cols = pl.ds(pl.multiple_of(m * 256, 256), 256)
            r = jnp.dot(a_ref[...], buf[n, 0], preferred_element_type=jnp.float32)
            r = r + jnp.dot(b_ref[...], buf[n, 1], preferred_element_type=jnp.float32)
            if received:
                r = r + rest[half][:, cols].astype(jnp.float32)
            outs[half][:, cols] = r.astype(outs[half].dtype)
            return carry

        lax.fori_loop(0, 2, one, 0)


def project(pieces, j, a, b, w, ws, recv=(), dtype=jnp.bfloat16):
    rows, depth = a.shape
    hbm = pl.BlockSpec(memory_space=pltpu.HBM)
    return pl.pallas_call(
        functools.partial(project_body, pieces=pieces, received=len(recv)),
        out_shape=[jax.ShapeDtypeStruct((rows, 512), dtype)] * 2,
        in_specs=[SM, VM, VM, hbm, hbm] + [VM] * len(recv),
        out_specs=[VM, VM],
        scratch_shapes=[pltpu.VMEM((4, 2, depth, 256), jnp.bfloat16), pltpu.SemaphoreType.DMA((4, 2))],
        compiler_params=pltpu.CompilerParams(vmem_limit_bytes=60 * MIB),
        cost_estimate=pl.CostEstimate(flops=4 * rows * depth * 1024, bytes_accessed=7 * MIB, transcendentals=0),
    )(j, a, b, w, ws, *recv)


def move(a, f):
    return lax.ppermute(a, "tp", [(j, f(j)) for j in range(8)])


def up(a):
    return move(a, lambda j: (j + 2) % 8)


def down(a):
    return move(a, lambda j: (j - 2) % 8)


def swap(a):
    return move(a, lambda j: j ^ 1)


def tail(att, weight, theirs):
    j = lax.axis_index("tp").reshape(1)
    other = swap(att)
    args = (j, att, other, weight, theirs)
    c2a, c2b = project(((2, 0), (2, 1)), *args)
    a2, b2 = up(c2a), down(c2b)
    c1b, c3a = project(((1, 1), (3, 0)), *args)
    u2, d2 = up(c1b), down(c3a)
    c1a, c3b = project(((1, 0), (3, 1)), *args, recv=(a2, b2))
    u1, d1 = up(c1a), down(c3b)
    left, right = project(((0, 0), (0, 1)), *args, recv=(d2, u2), dtype=jnp.float32)
    left = left + u1.astype(jnp.float32)
    right = right + d1.astype(jnp.float32)
    return jnp.concatenate([left, right], axis=1).astype(jnp.bfloat16)


def shards(queries, own_keys, own_values, cache_keys, cache_values, selected, out_weight):
    blocks_dev = cache_keys.shape[1] // R
    picked = selected[0, 0]
    owners = lax.axis_size("ctx")
    owner_of = picked // blocks_dev
    inside = picked % blocks_dev
    match = owner_of[:, None] == jnp.arange(owners, dtype=jnp.int32)[None, :]
    request = jnp.sum(jnp.where(match, inside[:, None], 0), axis=0)
    wanted = lax.all_to_all(request, "ctx", split_axis=0, concat_axis=0, tiled=True)
    send_a, send_b = gather(wanted, cache_keys.reshape(blocks_dev, R, W), cache_values.reshape(blocks_dev, R, W))
    got_a = lax.all_to_all(send_a, "ctx", split_axis=0, concat_axis=0, tiled=True)
    got_a, send_b = lax.optimization_barrier((got_a, send_b))
    got_b = lax.all_to_all(send_b, "ctx", split_axis=0, concat_axis=0, tiled=True)
    side = (1 - lax.axis_index("tp") % 2).reshape(1)
    theirs = sibling_columns(out_weight, side)
    theirs = swap(theirs)
    q = jnp.transpose(queries, (1, 0, 2))
    zero = jnp.zeros((1,), jnp.int32)
    state = attend(zero, q, (own_keys.reshape(R, W), own_values.reshape(R, W)), per=1, items=1, width=R, own=True)
    state = attend(owner_of, q, (got_a, *state), per=4, items=2, width=CUT)
    att = attend(owner_of, q, (got_b, *state), per=4, items=2, width=R - CUT, last=True)
    return tail(att, out_weight, theirs)


def solution(mesh):
    in_specs = (
        P("ctx", "tp", None),
        P("ctx", "tp", None),
        P("ctx", "tp", None),
        P("tp", "ctx", None),
        P("tp", "ctx", None),
        P("ctx", "tp", None),
        P("tp", None),
    )
    return jax.shard_map(shards, mesh=mesh, in_specs=in_specs, out_specs=P("ctx", "tp"), check_vma=False)
```

time: 195 us -> 160 us (0.82)
  waiting for transfers between devices: 97.3 us -> 39.7 us
  Pallas kernels: 35.1 us -> 73.7 us
  matrix products: 14.7 us -> 0 us
  between operations: 13.4 us -> 0.16 us
  starting transfers between devices: 11.1 us -> 22.3 us
    reduce_scatter x1 -> x0, waiting for transfers between devices: 53.1 us -> none  [shards(): return lax.psum_scatter(partial_term, 'tp', scatter_dimension=1, tiled=True)]
    pallas_call x2 -> x9, Pallas kernels: 35.1 us -> 73.7 us  [the longest x3 36.4 us: attend(): pl.pallas_call(functools.partial(attend_body, per=per, items=items, group...]
    dot_general x1 -> x0, matrix products: 14.7 us -> none  [shards(): jnp.dot(attended, out_weight, preferred_element_type=jnp.float32)]
    ppermute x0 -> x8, starting transfers between devices: none -> 14.1 us  [move(): return lax.ppermute(a, 'tp', [(j, f(j)) for j in range(8)])]
    all_to_all x2, waiting for transfers between devices: 44.1 us -> 31.3 us  [the longest x1 28.8 us: shards(): lax.all_to_all(send_a, 'ctx', split_axis=0, concat_axis=0, tiled=True)]
    ppermute x0 -> x8, waiting for transfers between devices: none -> 8.42 us  [move(): return lax.ppermute(a, 'tp', [(j, f(j)) for j in range(8)])]
    gather x2 -> x0, local copies, waits for them, and re-layouts: 4.32 us -> none  [the longest x1 2.17 us: shards(): flat_keys[wanted]]
    all_to_all x2, starting transfers between devices: 11 us -> 8.14 us  [the longest x1 4.4 us: shards(): lax.all_to_all(send_b, 'ctx', split_axis=0, concat_axis=0, tiled=True)]
  transfers between devices with their start and end apart: 3 -> 10, of which waited for: 3 -> 5; matrix products, arithmetic and copies ran while one was open for 2% -> 3% of each run, Pallas kernels for 4% -> 38%
where the time goes in v2:
time: 160 us; the launch traced here: 159 us
  Pallas kernels  73.7 us (46%)
  waiting for transfers between devices  39.7 us (25%)
  starting transfers between devices  22.3 us (14%)
  blocking collectives  13.1 us (8%)
  local copies, waits for them, and re-layouts  6.6 us (4%)
  other arithmetic  3.12 us (2%)
    pallas_call x3, Pallas kernels, attend(): pl.pallas_call(functools.partial(attend_body, per=per, items=items, group...  36.4 us
    all_to_all x1, waiting for transfers between devices, shards(): lax.all_to_all(send_a, 'ctx', split_axis=0, concat_axis=0, tiled=True)  28.8 us
    pallas_call x4, Pallas kernels, project(): pl.pallas_call(functools.partial(project_body, pieces=pieces, received=le...  26.8 us
    ppermute x8, starting transfers between devices, move(): return lax.ppermute(a, 'tp', [(j, f(j)) for j in range(8)])  14.1 us
    all_to_all x1, blocking collectives, shards(): lax.all_to_all(request, 'ctx', split_axis=0, concat_axis=0, tiled=True)  13.1 us
    ppermute x8, waiting for transfers between devices, move(): return lax.ppermute(a, 'tp', [(j, f(j)) for j in range(8)])  8.42 us
    pallas_call x1, Pallas kernels, sibling_columns(): pl.pallas_call(copy_body, grid_spec=pltpu.PrefetchScalarGridSpec(num_scal...  7.31 us
    unnamed x23, local copies, waits for them, and re-layouts  6.51 us
  transfers between devices with their start and end apart: 10, of which 5 were waited for; matrix products, arithmetic and copies ran while one was open for 3% of the time, Pallas kernels for 38%

profile of v2, /device:TPU:1, one launch (start us, length us, event | category | flops | bytes accessed | tf_op | source)
XLA Modules:
  0.0 158.6 jit_solution(5979506047057022499)
XLA Ops:
  0.0 7.3 %shard_map.77 = bf16[1024,4096]{1,0:T(8,128)(2,1)} custom-call(s32[1]{0:T(128)} %bitcast.8.ix_ref, bf16[1024,8192]{1,0:T(8,128)(2,1)} %w_ref.7), custom_call_target="tpu_custom_call" | custom-call | bytes 16777216 | tf_op jit(solution)/shard_map/pallas_call | solution.py:149
  7.3 1.4 collective-permute-start.1
  8.7 0.0 copy-done.9
  8.7 0.0 copy-start.10
  8.7 0.1 select_reduce_fusion
  8.8 0.1 copy.14
  8.9 13.1 %all_to_all.21 = s32[16,1,1]{2,1,0:T(1,128)S(1)} all-to-all(s32[16,1,1]{2,1,0:T(1,128)S(1)} %copy.14), channel_id=1, replica_groups=mesh['ctx'=16,'tp'=8] {'ctx'}, dimensions={0} | all-to-all | bytes 128 | tf_op jit(solution)/shard_map/all_to_all | solution.py:250
  22.0 0.4 reduce.want_ref
  22.4 0.0 copy-done
  22.4 0.0 copy-done.1
  22.4 3.1 %shard_map.73 = (bf16[16,2,320,128]{3,2,1,0:T(8,128)(2,1)}, bf16[16,2,192,128]{3,2,1,0:T(8,128)(2,1)}) custom-call(s32[16]{0:T(128)S(1)} %reduce.want_ref, bf16[8,512,128]{2,1,0:T(8,128)(2,1)S(1)} %bitcast.25, bf16[8,512,128]{2,1,0:T(8,128)(2,1)S(1)} %bitcast.26), custom_call_target="tpu_custom_call" | custom-call | bytes 8388608 | tf_op jit(solution)/shard_map/pallas_call | solution.py:129
  25.5 0.0 copy-done.10
  25.5 3.7 %all-to-all-start.1 = ((bf16[16,2,320,128]{3,2,1,0:T(8,128)(2,1)}), bf16[16,2,320,128]{3,2,1,0:T(8,128)(2,1)S(1)}, u32[]{:S(2)}, u32[]{:S(2)}) async-start(bf16[16,2,320,128]{3,2,1,0:T(8,128)(2,1)} %get-tuple-element.21), calls=%async_computation.1 | async-start | bytes 5242880 | tf_op jit(solution)/shard_map/all_to_all | solution.py:252
  29.3 2.3 %copy.16 = bf16[512,8,128]{2,0,1:T(8,128)(2,1)} copy(bf16[512,8,128]{2,1,0:T(8,128)(2,1)} %param.7) | data formatting | bytes 2097152 | tf_op args[0]
  31.6 6.0 %shard_map.74 = (f32[8,512,256]{2,1,0:T(8,128)}, f32[8,512,128]{2,1,0:T(8,128)}) custom-call(s32[1]{0:T(128)} %constant.45.clone.1.pos_ref, bf16[8,512,128]{2,1,0:T(8,128)(2,1)} %bitcast.27, bf16[512,128]{1,0:T(8,128)(2,1)} %bitcast.31, bf16[512,128]{1,0:T(8,128)(2,1)} %bitcast.32), custom_call_target="tpu_custom_call" | custom-call | flops 4294967296 | bytes 16777216 | tf_op jit(solution)/shard_map/pallas_call | solution.py:99
  37.6 28.8 %all-to-all-done.1.rest_0_ = bf16[16,2,320,128]{3,2,1,0:T(8,128)(2,1)S(1)} async-done(((bf16[16,2,320,128]{3,2,1,0:T(8,128)(2,1)}), bf16[16,2,320,128]{3,2,1,0:T(8,128)(2,1)S(1)}, u32[]{:S(2)}, u32[]{:S(2)}) %all-to-all-start.1) | async-done | bytes 2621472 | tf_op jit(solution)/shard_map/all_to_all | solution.py:252
  66.4 4.4 %all-to-all-start.2 = ((bf16[16,2,192,128]{3,2,1,0:T(8,128)(2,1)}), bf16[16,2,192,128]{3,2,1,0:T(8,128)(2,1)}, u32[]{:S(2)}, u32[]{:S(2)}) async-start(bf16[16,2,192,128]{3,2,1,0:T(8,128)(2,1)} %get-tuple-element.23), calls=%async_computation.2 | async-start | bytes 3145728 | tf_op jit(solution)/shard_map/all_to_all | solution.py:254
  70.8 0.0 copy-done.3
  70.8 17.5 %shard_map.75 = (f32[8,512,256]{2,1,0:T(8,128)}, f32[8,512,128]{2,1,0:T(8,128)}) custom-call(s32[8]{0:T(128)} %copy-done.10, bf16[8,512,128]{2,1,0:T(8,128)(2,1)} %bitcast.28, bf16[16,2,320,128]{3,2,1,0:T(8,128)(2,1)} %copy-done.3, f32[8,512,256]{2,1,0:T(8,128)} %get-tuple-element.25.rest_1_, f32[8,512,128]{2,1,0:T(8,128)} %get-tuple-element.26.rest_2_), custom_call_target="tpu_custom_call" | custom-call | flops 21474836480 | bytes 16777216 | tf_op jit(solution)/shard_map/pallas_call | solution.py:99
  88.4 2.5 %all-to-all-done.2.rest_0_ = bf16[16,2,192,128]{3,2,1,0:T(8,128)(2,1)} async-done(((bf16[16,2,192,128]{3,2,1,0:T(8,128)(2,1)}), bf16[16,2,192,128]{3,2,1,0:T(8,128)(2,1)}, u32[]{:S(2)}, u32[]{:S(2)}) %all-to-all-start.2) | async-done | bytes 1572896 | tf_op jit(solution)/shard_map/all_to_all | solution.py:254
  90.9 12.8 %shard_map.76.a_ref = bf16[512,1024]{1,0:T(8,128)(2,1)} custom-call(s32[8]{0:T(128)} %copy-done.10, bf16[8,512,128]{2,1,0:T(8,128)(2,1)} %bitcast.29, bf16[16,2,192,128]{3,2,1,0:T(8,128)(2,1)} %all-to-all-done.2.rest_0_, f32[8,512,256]{2,1,0:T(8,128)} %get-tuple-element.27.rest_1_, f32[8,512,128]{2,1,0:T(8,128)} %get-tuple-element.28.rest_2_), custom_call_target="tpu_custom_call" | custom-call | flops 12884901888 | bytes 16777216 | tf_op jit(solution)/shard_map/pallas_call | solution.py:99
  103.8 4.4 %collective-permute-start = (bf16[512,1024]{1,0:T(8,128)(2,1)}, bf16[512,1024]{1,0:T(8,128)(2,1)S(1)}, u32[]{:S(2)}, u32[]{:S(2)}) collective-permute-start(bf16[512,1024]{1,0:T(8,128)(2,1)} %shard_map.76.a_ref), channel_id=1, source_target_pairs={{0,1},{1,0},{2,3},{3,2},{4,5},{5,4},{6,7},{7,6},{8,9},{9,8},{10,11... | collective-permute-start | bytes 3145736 | tf_op jit(solution)/shard_map/ppermute | solution.py:211
  108.1 2.5 %collective-permute-done.b_ref = bf16[512,1024]{1,0:T(8,128)(2,1)S(1)} collective-permute-done((bf16[512,1024]{1,0:T(8,128)(2,1)}, bf16[512,1024]{1,0:T(8,128)(2,1)S(1)}, u32[]{:S(2)}, u32[]{:S(2)}) %collective-permute-start) | collective-permute-done | bytes 1048608 | tf_op jit(solution)/shard_map/ppermute | solution.py:211
  110.6 0.0 collective-permute-done.1.ws_ref
  110.6 1.0 copy-done.2
  111.6 6.5 %shard_map.80 = (bf16[512,512]{1,0:T(8,128)(2,1)}, bf16[512,512]{1,0:T(8,128)(2,1)}) custom-call(s32[1]{0:T(128)} %bitcast.j_ref, bf16[512,1024]{1,0:T(8,128)(2,1)} %shard_map.76.a_ref, bf16[512,1024]{1,0:T(8,128)(2,1)} %copy-done.2, bf16[1024,8192]{1,0:T(8,128)(2,1)} %w_ref.7, bf16[1024,4096]{1,0:T(8,128)(2,1)} %collective-permute-done.1.ws_ref), custom_call_target="tpu_custom_call" | custom-call | flops 2147483648 | bytes 7340032 | tf_op jit(solution)/shard_map/pallas_call | solution.py:199
  118.1 1.7 %collective-permute-start.4 = (bf16[512,512]{1,0:T(8,128)(2,1)}, bf16[512,512]{1,0:T(8,128)(2,1)S(1)}, u32[]{:S(2)}, u32[]{:S(2)}) collective-permute-start(bf16[512,512]{1,0:T(8,128)(2,1)} %get-tuple-element.32), channel_id=1, source_target_pairs={{0,2},{1,3},{2,4},{3,5},{4,6},{5,7},{6,0},{7,1},{8,10},{9,11},{10,... | collective-permute-start | bytes 1572872 | tf_op jit(solution)/shard_map/ppermute | solution.py:211
  119.8 2.4 %collective-permute-start.5 = (bf16[512,512]{1,0:T(8,128)(2,1)}, bf16[512,512]{1,0:T(8,128)(2,1)S(1)}, u32[]{:S(2)}, u32[]{:S(2)}) collective-permute-start(bf16[512,512]{1,0:T(8,128)(2,1)} %get-tuple-element.33), channel_id=1, source_target_pairs={{0,6},{1,7},{2,0},{3,1},{4,2},{5,3},{6,4},{7,5},{8,14},{9,15},{10,... | collective-permute-start | bytes 1572872 | tf_op jit(solution)/shard_map/ppermute | solution.py:211
  122.2 6.5 %shard_map.78 = (bf16[512,512]{1,0:T(8,128)(2,1)}, bf16[512,512]{1,0:T(8,128)(2,1)}) custom-call(s32[1]{0:T(128)} %bitcast.j_ref, bf16[512,1024]{1,0:T(8,128)(2,1)} %shard_map.76.a_ref, bf16[512,1024]{1,0:T(8,128)(2,1)} %copy-done.2, bf16[1024,8192]{1,0:T(8,128)(2,1)} %w_ref.7, bf16[1024,4096]{1,0:T(8,128)(2,1)} %collective-permute-done.1.ws_ref), custom_call_target="tpu_custom_call" | custom-call | flops 2147483648 | bytes 7340032 | tf_op jit(solution)/shard_map/pallas_call | solution.py:199
  128.7 1.3 collective-permute-start.2
  129.9 0.3 collective-permute-start.3
  130.2 3.8 %collective-permute-done.4.rest_0_ = bf16[512,512]{1,0:T(8,128)(2,1)S(1)} collective-permute-done((bf16[512,512]{1,0:T(8,128)(2,1)}, bf16[512,512]{1,0:T(8,128)(2,1)S(1)}, u32[]{:S(2)}, u32[]{:S(2)}) %collective-permute-start.4) | collective-permute-done | bytes 524320 | tf_op jit(solution)/shard_map/ppermute | solution.py:211
  134.1 0.0 collective-permute-done.5.rest_1_
  134.1 0.8 copy-done.7
  134.9 0.8 copy-done.8
  135.7 6.8 %shard_map.81 = (bf16[512,512]{1,0:T(8,128)(2,1)}, bf16[512,512]{1,0:T(8,128)(2,1)}) custom-call(s32[1]{0:T(128)} %bitcast.j_ref, bf16[512,1024]{1,0:T(8,128)(2,1)} %shard_map.76.a_ref, bf16[512,1024]{1,0:T(8,128)(2,1)} %copy-done.2, bf16[1024,8192]{1,0:T(8,128)(2,1)} %w_ref.7, bf16[1024,4096]{1,0:T(8,128)(2,1)} %collective-permute-done.1.ws_ref, ...), custom_call_target="tpu_custom_call" | custom-call | flops 2147483648 | bytes 7340032 | tf_op jit(solution)/shard_map/pallas_call | solution.py:199
  142.5 0.1 collective-permute-start.6
  142.5 2.7 %collective-permute-start.7 = (bf16[512,512]{1,0:T(8,128)(2,1)}, bf16[512,512]{1,0:T(8,128)(2,1)S(1)}, u32[]{:S(2)}, u32[]{:S(2)}) collective-permute-start(bf16[512,512]{1,0:T(8,128)(2,1)} %get-tuple-element.36), channel_id=1, source_target_pairs={{0,6},{1,7},{2,0},{3,1},{4,2},{5,3},{6,4},{7,5},{8,14},{9,15},{10,... | collective-permute-start | bytes 1572872 | tf_op jit(solution)/shard_map/ppermute | solution.py:211
  145.2 0.0 collective-permute-done.2.rest_0_
  145.2 0.0 collective-permute-done.3.rest_1_
  145.2 0.8 copy-done.5
  146.0 0.8 copy-done.6
  146.8 7.0 %shard_map.79 = (f32[512,512]{1,0:T(8,128)}, f32[512,512]{1,0:T(8,128)}) custom-call(s32[1]{0:T(128)} %bitcast.j_ref, bf16[512,1024]{1,0:T(8,128)(2,1)} %shard_map.76.a_ref, bf16[512,1024]{1,0:T(8,128)(2,1)} %copy-done.2, bf16[1024,8192]{1,0:T(8,128)(2,1)} %w_ref.7, bf16[1024,4096]{1,0:T(8,128)(2,1)} %collective-permute-done.1.ws_ref, ...), custom_call_target="tpu_custom_call" | custom-call | flops 2147483648 | bytes 7340032 | tf_op jit(solution)/shard_map/pallas_call | solution.py:199
  153.9 2.1 %collective-permute-done.6 = bf16[512,512]{1,0:T(8,128)(2,1)S(1)} collective-permute-done((bf16[512,512]{1,0:T(8,128)(2,1)}, bf16[512,512]{1,0:T(8,128)(2,1)S(1)}, u32[]{:S(2)}, u32[]{:S(2)}) %collective-permute-start.6) | collective-permute-done | bytes 524320 | tf_op jit(solution)/shard_map/ppermute | solution.py:211
  155.9 1.4 add_convert_fusion.1
  157.3 0.0 collective-permute-done.7
  157.4 0.2 add_convert_fusion
  157.5 1.1 pad_maximum_fusion
  (12 shorter events, 0.0 us)
Async XLA Ops:
  0.0 8.7 %copy-start.9 = (s32[1,1,8]{2,1,0:T(1,128)S(1)}, s32[1,1,8]{2,1,0:T(1,128)}, u32[]{:S(2)}) copy-start(s32[1,1,8]{2,1,0:T(1,128)} %param.12) | copy-start | bytes 100
  0.0 22.4 %copy-start = (bf16[1,4096,128]{2,1,0:T(8,128)(2,1)S(1)}, bf16[1,4096,128]{2,1,0:T(8,128)(2,1)}, u32[]{:S(2)}) copy-start(bf16[1,4096,128]{2,1,0:T(8,128)(2,1)} %param.10) | copy-start | bytes 3145732
  0.0 22.4 %copy-start.1 = (bf16[1,4096,128]{2,1,0:T(8,128)(2,1)S(1)}, bf16[1,4096,128]{2,1,0:T(8,128)(2,1)}, u32[]{:S(2)}) copy-start(bf16[1,4096,128]{2,1,0:T(8,128)(2,1)} %param.11) | copy-start | bytes 3145732
  7.3 103.3 %collective-permute-start.1 = (bf16[1024,4096]{1,0:T(8,128)(2,1)}, bf16[1024,4096]{1,0:T(8,128)(2,1)}, u32[]{:S(2)}, u32[]{:S(2)}) collective-permute-start(bf16[1024,4096]{1,0:T(8,128)(2,1)} %shard_map.77), channel_id=1, source_target_pairs={{0,1},{1,0},{2,3},{3,2},{4,5},{5,4},{6,7},{7,6},{8,9},{9,8},{10,11... | collective-permute-start | bytes 25165832 | tf_op jit(solution)/shard_map/ppermute | solution.py:211
  8.7 16.8 %copy-start.10 = (s32[8]{0:T(128)}, s32[8]{0:T(128)S(1)}, u32[]{:S(2)}) copy-start(s32[8]{0:T(128)S(1)} %get-tuple-element.38.pos_ref) | copy-start | bytes 100
  25.5 40.9 %all-to-all-start.1 = ((bf16[16,2,320,128]{3,2,1,0:T(8,128)(2,1)}), bf16[16,2,320,128]{3,2,1,0:T(8,128)(2,1)S(1)}, u32[]{:S(2)}, u32[]{:S(2)}) async-start(bf16[16,2,320,128]{3,2,1,0:T(8,128)(2,1)} %get-tuple-element.21), calls=%async_computation.1 | async-start | bytes 5242880 | tf_op jit(solution)/shard_map/all_to_all | solution.py:252
  66.4 4.4 %copy-start.3 = (bf16[16,2,320,128]{3,2,1,0:T(8,128)(2,1)}, bf16[16,2,320,128]{3,2,1,0:T(8,128)(2,1)S(1)}, u32[]{:S(2)}) copy-start(bf16[16,2,320,128]{3,2,1,0:T(8,128)(2,1)S(1)} %all-to-all-done.1.rest_0_) | copy-start | bytes 7864324
  66.4 24.5 %all-to-all-start.2 = ((bf16[16,2,192,128]{3,2,1,0:T(8,128)(2,1)}), bf16[16,2,192,128]{3,2,1,0:T(8,128)(2,1)}, u32[]{:S(2)}, u32[]{:S(2)}) async-start(bf16[16,2,192,128]{3,2,1,0:T(8,128)(2,1)} %get-tuple-element.23), calls=%async_computation.2 | async-start | bytes 3145728 | tf_op jit(solution)/shard_map/all_to_all | solution.py:254
  103.8 6.9 %collective-permute-start = (bf16[512,1024]{1,0:T(8,128)(2,1)}, bf16[512,1024]{1,0:T(8,128)(2,1)S(1)}, u32[]{:S(2)}, u32[]{:S(2)}) collective-permute-start(bf16[512,1024]{1,0:T(8,128)(2,1)} %shard_map.76.a_ref), channel_id=1, source_target_pairs={{0,1},{1,0},{2,3},{3,2},{4,5},{5,4},{6,7},{7,6},{8,9},{9,8},{10,11... | collective-permute-start | bytes 3145736 | tf_op jit(solution)/shard_map/ppermute | solution.py:211
  110.6 1.0 copy-start.2
  118.1 16.0 %collective-permute-start.4 = (bf16[512,512]{1,0:T(8,128)(2,1)}, bf16[512,512]{1,0:T(8,128)(2,1)S(1)}, u32[]{:S(2)}, u32[]{:S(2)}) collective-permute-start(bf16[512,512]{1,0:T(8,128)(2,1)} %get-tuple-element.32), channel_id=1, source_target_pairs={{0,2},{1,3},{2,4},{3,5},{4,6},{5,7},{6,0},{7,1},{8,10},{9,11},{10,... | collective-permute-start | bytes 1572872 | tf_op jit(solution)/shard_map/ppermute | solution.py:211
  119.8 14.3 %collective-permute-start.5 = (bf16[512,512]{1,0:T(8,128)(2,1)}, bf16[512,512]{1,0:T(8,128)(2,1)S(1)}, u32[]{:S(2)}, u32[]{:S(2)}) collective-permute-start(bf16[512,512]{1,0:T(8,128)(2,1)} %get-tuple-element.33), channel_id=1, source_target_pairs={{0,6},{1,7},{2,0},{3,1},{4,2},{5,3},{6,4},{7,5},{8,14},{9,15},{10,... | collective-permute-start | bytes 1572872 | tf_op jit(solution)/shard_map/ppermute | solution.py:211
  128.7 16.5 %collective-permute-start.2 = (bf16[512,512]{1,0:T(8,128)(2,1)}, bf16[512,512]{1,0:T(8,128)(2,1)S(1)}, u32[]{:S(2)}, u32[]{:S(2)}) collective-permute-start(bf16[512,512]{1,0:T(8,128)(2,1)} %get-tuple-element.29), channel_id=1, source_target_pairs={{0,6},{1,7},{2,0},{3,1},{4,2},{5,3},{6,4},{7,5},{8,14},{9,15},{10,... | collective-permute-start | bytes 1572872 | tf_op jit(solution)/shard_map/ppermute | solution.py:211
  129.9 15.3 %collective-permute-start.3 = (bf16[512,512]{1,0:T(8,128)(2,1)}, bf16[512,512]{1,0:T(8,128)(2,1)S(1)}, u32[]{:S(2)}, u32[]{:S(2)}) collective-permute-start(bf16[512,512]{1,0:T(8,128)(2,1)} %get-tuple-element.30), channel_id=1, source_target_pairs={{0,2},{1,3},{2,4},{3,5},{4,6},{5,7},{6,0},{7,1},{8,10},{9,11},{10,... | collective-permute-start | bytes 1572872 | tf_op jit(solution)/shard_map/ppermute | solution.py:211
  134.1 0.8 copy-start.7
  134.9 0.8 copy-start.8
  142.5 13.5 %collective-permute-start.6 = (bf16[512,512]{1,0:T(8,128)(2,1)}, bf16[512,512]{1,0:T(8,128)(2,1)S(1)}, u32[]{:S(2)}, u32[]{:S(2)}) collective-permute-start(bf16[512,512]{1,0:T(8,128)(2,1)} %get-tuple-element.34), channel_id=1, source_target_pairs={{0,2},{1,3},{2,4},{3,5},{4,6},{5,7},{6,0},{7,1},{8,10},{9,11},{10,... | collective-permute-start | bytes 1572872 | tf_op jit(solution)/shard_map/ppermute | solution.py:211
  142.5 14.8 %collective-permute-start.7 = (bf16[512,512]{1,0:T(8,128)(2,1)}, bf16[512,512]{1,0:T(8,128)(2,1)S(1)}, u32[]{:S(2)}, u32[]{:S(2)}) collective-permute-start(bf16[512,512]{1,0:T(8,128)(2,1)} %get-tuple-element.36), channel_id=1, source_target_pairs={{0,6},{1,7},{2,0},{3,1},{4,2},{5,3},{6,4},{7,5},{8,14},{9,15},{10,... | collective-permute-start | bytes 1572872 | tf_op jit(solution)/shard_map/ppermute | solution.py:211
  145.2 0.8 copy-start.5
  146.0 0.8 copy-start.6
  153.9 3.5 %copy-start.4 = (f32[512,512]{1,0:T(8,128)S(1)}, f32[512,512]{1,0:T(8,128)}, u32[]{:S(2)}) copy-start(f32[512,512]{1,0:T(8,128)} %get-tuple-element.35) | copy-start | bytes 3145732
